TPU v7x, 32 devices: a whole 2x2x4 slice. The times are simulated.
32 devices in a mesh: trial: 4 (over x, core), north: 2 (over y), east: 4 (over z).
Axes of the slice: x: 2, y: 2, z: 4, core: 2. Of those that a mesh axis runs over, the one named last changes fastest.
Arguments:
- pair_state: bfloat16 [192, 48, 128], P(('trial', 'north'), 'east'), parts along dimension 0, may hold values from -6 to 6
- in_gain: float32 [128], replicated, may hold values from 0.25 to 1.75
- left_weight: bfloat16 [512, 128], P('trial'), parts along dimension 0, may hold values from -0.5 to 0.5
- right_weight: bfloat16 [512, 128], P('trial'), parts along dimension 0, may hold values from -0.5 to 0.5
- left_gate: bfloat16 [512, 128], P('trial'), parts along dimension 0, may hold values from -0.5 to 0.5
- right_gate: bfloat16 [512, 128], P('trial'), parts along dimension 0, may hold values from -0.5 to 0.5
- mid_gain: float32 [128], replicated, may hold values from 0.25 to 1.75
- out_weight: bfloat16 [512, 128], P('trial'), parts along dimension 0, may hold values from -0.5 to 0.5
- out_gate: bfloat16 [512, 128], P('trial'), parts along dimension 0, may hold values from -0.5 to 0.5
Outputs:
- triangle_out: bfloat16 [192, 48, 128], P(('trial', 'north'), 'east'), parts along dimension 0
There are 4 independent parts, one for each index of `trial`. A program takes and returns all parts, laid end to end along the dimension named above; an argument that names none is the same for every part. Nothing has to cross between parts.
All inputs are finite; a program needn't handle non-finite values.
Results may differ from a plain program's by a relative error of at most 0.015.
Values may be sent and summed in bfloat16 or wider, within the bound.
A program may use at most 64 MiB of HBM per device.

v0:
```python
import jax
import jax.numpy as jnp
from jax import lax
from jax.sharding import PartitionSpec as P


def norm_channels(values, channel_gain):
    centred = values - jnp.mean(values, axis=-1, keepdims=True)
    return (
        centred
        * lax.rsqrt(jnp.mean(centred * centred, axis=-1, keepdims=True) + 1e-05)
        * channel_gain
    )


def make_factors(pair_in, in_gain, left_weight, right_weight, left_gate, right_gate):
    ready = norm_channels(pair_in.astype(jnp.float32), in_gain).astype(jnp.bfloat16)
    ready = lax.optimization_barrier(ready)
    left = jnp.einsum("ijc,cd->ijd", ready, left_weight, preferred_element_type=jnp.float32)
    left = left * jax.nn.sigmoid(
        jnp.einsum("ijc,cd->ijd", ready, left_gate, preferred_element_type=jnp.float32)
    )
    right = jnp.einsum("ijc,cd->ijd", ready, right_weight, preferred_element_type=jnp.float32)
    right = right * jax.nn.sigmoid(
        jnp.einsum("ijc,cd->ijd", ready, right_gate, preferred_element_type=jnp.float32)
    )
    return (ready, left.astype(jnp.bfloat16), right.astype(jnp.bfloat16))


def to_pair(mixed, ready, mid_gain, out_weight, out_gate):
    scaled = norm_channels(mixed.astype(jnp.float32), mid_gain).astype(jnp.bfloat16)
    scaled = lax.optimization_barrier(scaled)
    gate = jax.nn.sigmoid(
        jnp.einsum("ijc,cd->ijd", ready, out_gate, preferred_element_type=jnp.float32)
    )
    return (
        jnp.einsum("ijd,dc->ijc", scaled, out_weight, preferred_element_type=jnp.float32) * gate
    ).astype(jnp.bfloat16)


def local(
    pair_state,
    in_gain,
    left_weight,
    right_weight,
    left_gate,
    right_gate,
    mid_gain,
    out_weight,
    out_gate,
):
    ready, left, right = make_factors(
        pair_state, in_gain, left_weight, right_weight, left_gate, right_gate
    )
    count = pair_state.shape[1] * lax.axis_size("east")
    left_lines, right_lines = (
        lax.all_to_all(left, "east", split_axis=2, concat_axis=1, tiled=True),
        lax.all_to_all(right, "east", split_axis=2, concat_axis=1, tiled=True),
    )
    strip = jnp.einsum(
        "ikd,jkd->ijd",
        left_lines,
        lax.all_gather(right_lines, "north", axis=0, tiled=True),
        preferred_element_type=jnp.float32,
    )
    strip = (strip * count ** (-0.5)).astype(jnp.bfloat16)
    mixed = lax.all_to_all(strip, "east", split_axis=1, concat_axis=2, tiled=True)
    return to_pair(mixed, ready, mid_gain, out_weight, out_gate)


def solution(mesh):
    return jax.shard_map(
        local,
        mesh=mesh,
        in_specs=(
            P(("trial", "north"), "east", None),
            P(),
            P("trial", None),
            P("trial", None),
            P("trial", None),
            P("trial", None),
            P(),
            P("trial", None),
            P("trial", None),
        ),
        out_specs=P(("trial", "north"), "east", None),
        check_vma=False,
    )
```

profile of v0, /device:TPU:0, one launch (start us, length us, event | category | flops | bytes accessed | tf_op | source)
XLA Modules:
  0.0 44.6 jit_solution(821063206014544712)
XLA Ops:
  0.0 1.1 %convert_reduce_fusion = f32[24,12]{0,1:T(8,128)S(1)} fusion(bf16[24,12,128]{2,0,1:T(8,128)(2,1)} %param.9), kind=kLoop, calls=%fused_computation.25 | loop fusion | flops 73440 | bytes 74880 | tf_op jit(solution)/shard_map/reduce_sum | solution.py:8
  1.3 0.6 %copy-done.4 = f32[128]{0:T(128)S(1)} copy-done((f32[128]{0:T(128)S(1)}, f32[128]{0:T(128)}, u32[]{:S(2)}) %copy-start.4) | copy-done | bytes 536
  2.3 0.6 %copy-done.6 = bf16[128,128]{1,0:T(8,128)(2,1)S(1)} copy-done((bf16[128,128]{1,0:T(8,128)(2,1)S(1)}, bf16[128,128]{1,0:T(8,128)(2,1)}, u32[]{:S(2)}) %copy-start.6) | copy-done | bytes 32792
  2.9 0.2 fusion.16
  3.1 0.4 copy.34
  3.5 1.1 %reshape.41 = bf16[4,2,4608]{2,1,0:T(2,128)(2,1)} reshape(bf16[128,12,24]{2,1,0:T(8,128)(2,1)S(1)} %bitcast.55) | data formatting | bytes 147456
  4.7 6.5 %all-to-all-start = ((bf16[4,2,4608]{2,1,0:T(2,128)(2,1)}), bf16[4,2,4608]{2,1,0:T(2,128)(2,1)S(1)}, u32[]{:S(2)}, u32[]{:S(2)}) async-start(bf16[4,2,4608]{2,1,0:T(2,128)(2,1)} %reshape.41), calls=%async_computation | async-start | bytes 147456 | tf_op jit(solution)/shard_map/all_to_all | solution.py:58
  11.3 0.6 %copy-done.7 = bf16[128,128]{1,0:T(8,128)(2,1)S(1)} copy-done((bf16[128,128]{1,0:T(8,128)(2,1)S(1)}, bf16[128,128]{1,0:T(8,128)(2,1)}, u32[]{:S(2)}) %copy-start.7) | copy-done | bytes 32792
  11.9 0.2 fusion.15
  12.1 0.4 copy.37
  12.5 1.1 %reshape.43 = bf16[4,2,4608]{2,1,0:T(2,128)(2,1)} reshape(bf16[128,12,24]{2,1,0:T(8,128)(2,1)S(1)} %bitcast.56) | data formatting | bytes 147456
  13.7 3.2 %all-to-all-done = bf16[4,2,4608]{2,1,0:T(2,128)(2,1)S(1)} async-done(((bf16[4,2,4608]{2,1,0:T(2,128)(2,1)}), bf16[4,2,4608]{2,1,0:T(2,128)(2,1)S(1)}, u32[]{:S(2)}, u32[]{:S(2)}) %all-to-all-start) | async-done | bytes 73760 | tf_op jit(solution)/shard_map/all_to_all | solution.py:58
  16.9 3.3 %all-to-all-start.1 = ((bf16[4,2,4608]{2,1,0:T(2,128)(2,1)}), bf16[4,2,4608]{2,1,0:T(2,128)(2,1)S(1)}, u32[]{:S(2)}, u32[]{:S(2)}) async-start(bf16[4,2,4608]{2,1,0:T(2,128)(2,1)} %reshape.43), calls=%async_computation.1 | async-start | bytes 147456 | tf_op jit(solution)/shard_map/all_to_all | solution.py:57
  20.2 0.6 %reshape.42 = bf16[128,12,24]{2,1,0:T(8,128)(2,1)S(1)} reshape(bf16[4,2,4608]{2,1,0:T(2,128)(2,1)S(1)} %all-to-all-done) | data formatting | bytes 147456
  20.8 0.4 copy.35
  21.2 0.3 copy.36
  21.5 6.3 %all_gather.3 = bf16[48,48,32]{1,0,2:T(8,128)(2,1)S(1)} all-gather(bf16[24,48,32]{1,0,2:T(8,128)(2,1)S(1)} %copy.36), channel_id=1, replica_groups=mesh['trial'=4,'north'=2,'east'=4] {'north'}, dimensions={0}, use_global_device_ids=true | all-gather | bytes 221184 | tf_op jit(solution)/shard_map/all_gather | solution.py:63
  27.8 0.6 %reshape.44 = bf16[128,12,24]{2,1,0:T(8,128)(2,1)S(1)} reshape(bf16[4,2,4608]{2,1,0:T(2,128)(2,1)S(1)} %all-to-all-done.1) | data formatting | bytes 147456
  28.4 0.4 copy.38
  28.8 0.3 copy.39
  29.1 0.3 fusion.1
  29.4 0.2 copy.40
  29.6 0.3 reshape.45
  29.9 10.6 %all_to_all.45 = bf16[4,2,4608]{2,1,0:T(2,128)(2,1)S(1)} all-to-all(bf16[4,2,4608]{2,1,0:T(2,128)(2,1)S(1)} %reshape.45), channel_id=1, replica_groups=mesh['trial'=4,'north'=2,'east'=4] {'east'}, dimensions={0} | all-to-all | bytes 147456 | tf_op jit(solution)/shard_map/all_to_all | solution.py:67
  40.5 0.2 reshape.46
  40.9 0.2 multiply_reduce_fusion
  41.2 0.4 copy.41
  41.6 0.3 reshape.32
  41.9 0.4 copy-done.5
  42.4 0.6 %copy-done.3 = bf16[128,128]{1,0:T(8,128)(2,1)S(1)} copy-done((bf16[128,128]{1,0:T(8,128)(2,1)S(1)}, bf16[128,128]{1,0:T(8,128)(2,1)}, u32[]{:S(2)}) %copy-start.3) | copy-done | bytes 32792
  43.2 0.6 %copy-done.8 = bf16[128,128]{1,0:T(8,128)(2,1)S(1)} copy-done((bf16[128,128]{1,0:T(8,128)(2,1)S(1)}, bf16[128,128]{1,0:T(8,128)(2,1)}, u32[]{:S(2)}) %copy-start.8) | copy-done | bytes 32792
  43.7 0.8 %fusion.14 = bf16[24,12,128]{2,0,1:T(8,128)(2,1)} fusion(f32[24,12,128]{2,0,1:T(8,128)S(1)} %fusion.24, bf16[24,12,128]{2,0,1:T(8,128)(2,1)S(1)} %fusion.22, bf16[128,128]{1,0:T(8,128)(2,1)S(1)} %copy-done.8), kind=kOutput, calls=%fused_computation.18 | convolution fusion | flops 9621504 | bytes 327680 | tf_op jit(solution)/shard_map/ijc,cd->ijd/dot_general | solution.py:34
  (25 shorter events, 1.2 us)
Async XLA Ops:
  0.0 2.1 %copy-start = (bf16[128,128]{1,0:T(8,128)(2,1)S(1)}, bf16[128,128]{1,0:T(8,128)(2,1)}, u32[]{:S(2)}) copy-start(bf16[128,128]{1,0:T(8,128)(2,1)} %param.12) | copy-start | bytes 98308
  0.0 1.1 %copy-start.1 = (bf16[24,12,128]{2,0,1:T(8,128)(2,1)S(1)}, bf16[24,12,128]{2,0,1:T(8,128)(2,1)}, u32[]{:S(2)}) copy-start(bf16[24,12,128]{2,0,1:T(8,128)(2,1)} %param.9) | copy-start | bytes 221188
  1.3 0.7 %copy-start.4 = (f32[128]{0:T(128)S(1)}, f32[128]{0:T(128)}, u32[]{:S(2)}) copy-start(f32[128]{0:T(128)} %param.10) | copy-start | bytes 1540
  2.1 0.8 %copy-start.6 = (bf16[128,128]{1,0:T(8,128)(2,1)S(1)}, bf16[128,128]{1,0:T(8,128)(2,1)}, u32[]{:S(2)}) copy-start(bf16[128,128]{1,0:T(8,128)(2,1)} %param.14) | copy-start | bytes 98308
  4.7 6.5 %copy-start.2 = (bf16[128,128]{1,0:T(8,128)(2,1)S(1)}, bf16[128,128]{1,0:T(8,128)(2,1)}, u32[]{:S(2)}) copy-start(bf16[128,128]{1,0:T(8,128)(2,1)} %param.11) | copy-start | bytes 98308
  4.7 12.2 %all-to-all-start = ((bf16[4,2,4608]{2,1,0:T(2,128)(2,1)}), bf16[4,2,4608]{2,1,0:T(2,128)(2,1)S(1)}, u32[]{:S(2)}, u32[]{:S(2)}) async-start(bf16[4,2,4608]{2,1,0:T(2,128)(2,1)} %reshape.41), calls=%async_computation | async-start | bytes 147456 | tf_op jit(solution)/shard_map/all_to_all | solution.py:58
  11.1 0.8 %copy-start.7 = (bf16[128,128]{1,0:T(8,128)(2,1)S(1)}, bf16[128,128]{1,0:T(8,128)(2,1)}, u32[]{:S(2)}) copy-start(bf16[128,128]{1,0:T(8,128)(2,1)} %param.13) | copy-start | bytes 98308
  16.9 10.9 %all-to-all-start.1 = ((bf16[4,2,4608]{2,1,0:T(2,128)(2,1)}), bf16[4,2,4608]{2,1,0:T(2,128)(2,1)S(1)}, u32[]{:S(2)}, u32[]{:S(2)}) async-start(bf16[4,2,4608]{2,1,0:T(2,128)(2,1)} %reshape.43), calls=%async_computation.1 | async-start | bytes 147456 | tf_op jit(solution)/shard_map/all_to_all | solution.py:57
  41.6 0.7 %copy-start.5 = (f32[128]{0:T(128)S(1)}, f32[128]{0:T(128)}, u32[]{:S(2)}) copy-start(f32[128]{0:T(128)} %param.15) | copy-start | bytes 1540
  42.2 0.8 %copy-start.3 = (bf16[128,128]{1,0:T(8,128)(2,1)S(1)}, bf16[128,128]{1,0:T(8,128)(2,1)}, u32[]{:S(2)}) copy-start(bf16[128,128]{1,0:T(8,128)(2,1)} %param.16) | copy-start | bytes 98308
  43.0 0.8 %copy-start.8 = (bf16[128,128]{1,0:T(8,128)(2,1)S(1)}, bf16[128,128]{1,0:T(8,128)(2,1)}, u32[]{:S(2)}) copy-start(bf16[128,128]{1,0:T(8,128)(2,1)} %param.17) | copy-start | bytes 98308
where the time goes:
time: 45.3 us; the launch traced here: 44.6 us
  blocking collectives  17 us (38%)
  local copies, waits for them, and re-layouts  10.4 us (23%)
  starting transfers between devices  9.77 us (22%)
  waiting for transfers between devices  3.24 us (7%)
  matrix products  2.02 us (4%)
  other arithmetic  1.96 us (4%)
    all_to_all x1, blocking collectives, local(): lax.all_to_all(strip, 'east', split_axis=1, concat_axis=2, tiled=True)  10.6 us
    unnamed x24, local copies, waits for them, and re-layouts  7.31 us
    all_to_all x1, starting transfers between devices, local(): lax.all_to_all(right, 'east', split_axis=2, concat_axis=1, tiled=True)  6.48 us
    all_gather x1, blocking collectives, local(): lax.all_gather(right_lines, 'north', axis=0, tiled=True)  6.34 us
    all_to_all x1, starting transfers between devices, local(): lax.all_to_all(left, 'east', split_axis=2, concat_axis=1, tiled=True)  3.29 us
    all_to_all x1, waiting for transfers between devices, local(): lax.all_to_all(right, 'east', split_axis=2, concat_axis=1, tiled=True)  3.23 us
    reduce_sum x2, other arithmetic, norm_channels(): centred = values - jnp.mean(values, axis=-1, keepdims=True)  1.19 us
  transfers between devices with their start and end apart: 2, of which 1 were waited for; matrix products, arithmetic and copies ran while one was open for 7% of the time, Pallas kernels for 0%

commit v1 on v0

--- a/solution.py
+++ b/solution.py
@@ -2,6 +2,18 @@
 import jax.numpy as jnp
 from jax import lax
 from jax.sharding import PartitionSpec as P
+
+
+def cut_along(shard, dim, peers):
+    shape = shard.shape
+    blocks = shard.reshape(*shape[:dim], peers, shape[dim] // peers, *shape[dim + 1 :])
+    return jnp.moveaxis(blocks, dim, 0)
+
+
+def joined_along(blocks, dim):
+    shape = list(blocks.shape[1:])
+    shape[dim] *= blocks.shape[0]
+    return jnp.moveaxis(blocks, 0, dim).reshape(shape)
 
 
 def norm_channels(values, channel_gain):
@@ -64,7 +76,14 @@
         preferred_element_type=jnp.float32,
     )
     strip = (strip * count ** (-0.5)).astype(jnp.bfloat16)
-    mixed = lax.all_to_all(strip, "east", split_axis=1, concat_axis=2, tiled=True)
+    size, index = (lax.axis_size("east"), lax.axis_index("east"))
+    parts = cut_along(strip, 1, size)
+    done = [parts[index]]
+    for turn in range(1, size):
+        sent = parts[(index + turn) % size]
+        done.append(lax.ppermute(sent, "east", [(i, (i + turn) % size) for i in range(size)]))
+    parts = jnp.stack(done)[(index - jnp.arange(size)) % size]
+    mixed = joined_along(parts, 2)
     return to_pair(mixed, ready, mid_gain, out_weight, out_gate)
 
 

time: 45.3 us -> 43.7 us (0.965)
  blocking collectives: 17 us -> 6.34 us
  starting transfers between devices: 9.77 us -> 15.6 us
  waiting for transfers between devices: 3.24 us -> 6.07 us
    all_to_all x1 -> x0, blocking collectives: 10.6 us -> none  [local(): lax.all_to_all(strip, 'east', split_axis=1, concat_axis=2, tiled=True)]
    ppermute x0 -> x3, starting transfers between devices: none -> 5.86 us  [local(): lax.ppermute(sent, 'east', [(i, (i + turn) % size) for i in range(size)])]
    ppermute x0 -> x3, waiting for transfers between devices: none -> 2.89 us  [local(): lax.ppermute(sent, 'east', [(i, (i + turn) % size) for i in range(size)])]
    gather x0 -> x1, local copies, waits for them, and re-layouts: none -> 0.6 us  [local(): parts = jnp.stack(done)[(index - jnp.arange(size)) % size]]
    unnamed x24 -> x22, local copies, waits for them, and re-layouts: 7.31 us -> 6.87 us
  transfers between devices with their start and end apart: 2 -> 5, of which waited for: 1 -> 4; matrix products, arithmetic and copies ran while one was open for 7% -> 7% of each run, Pallas kernels for 0% -> 0%
where the time goes in v1:
time: 43.7 us; the launch traced here: 43 us
  starting transfers between devices  15.6 us (36%)
  local copies, waits for them, and re-layouts  10.6 us (24%)
  blocking collectives  6.34 us (15%)
  waiting for transfers between devices  6.07 us (14%)
  other arithmetic  2.06 us (5%)
  matrix products  2.02 us (5%)
    unnamed x22, local copies, waits for them, and re-layouts  6.87 us
    all_to_all x1, starting transfers between devices, local(): lax.all_to_all(right, 'east', split_axis=2, concat_axis=1, tiled=True)  6.48 us
    all_gather x1, blocking collectives, local(): lax.all_gather(right_lines, 'north', axis=0, tiled=True)  6.34 us
    ppermute x3, starting transfers between devices, local(): lax.ppermute(sent, 'east', [(i, (i + turn) % size) for i in range(size)])  5.86 us
    all_to_all x1, starting transfers between devices, local(): lax.all_to_all(left, 'east', split_axis=2, concat_axis=1, tiled=True)  3.29 us
    all_to_all x1, waiting for transfers between devices, local(): lax.all_to_all(right, 'east', split_axis=2, concat_axis=1, tiled=True)  3.18 us
    ppermute x3, waiting for transfers between devices, local(): lax.ppermute(sent, 'east', [(i, (i + turn) % size) for i in range(size)])  2.89 us
    reduce_sum x2, other arithmetic, norm_channels(): centred = values - jnp.mean(values, axis=-1, keepdims=True)  1.19 us
  transfers between devices with their start and end apart: 5, of which 4 were waited for; matrix products, arithmetic and copies ran while one was open for 7% of the time, Pallas kernels for 0%

profile of v1, /device:TPU:0, one launch (start us, length us, event | category | flops | bytes accessed | tf_op | source)
XLA Modules:
  0.0 43.0 jit_solution(16770071728931304289)
XLA Ops:
  0.0 1.1 %convert_reduce_fusion = f32[24,12]{0,1:T(8,128)S(1)} fusion(bf16[24,12,128]{2,0,1:T(8,128)(2,1)} %param.9), kind=kLoop, calls=%fused_computation.27 | loop fusion | flops 73440 | bytes 74880 | tf_op jit(solution)/shard_map/reduce_sum | solution.py:20
  1.3 0.6 %copy-done.4 = f32[128]{0:T(128)S(1)} copy-done((f32[128]{0:T(128)S(1)}, f32[128]{0:T(128)}, u32[]{:S(2)}) %copy-start.4) | copy-done | bytes 536
  2.3 0.6 %copy-done.6 = bf16[128,128]{1,0:T(8,128)(2,1)S(1)} copy-done((bf16[128,128]{1,0:T(8,128)(2,1)S(1)}, bf16[128,128]{1,0:T(8,128)(2,1)}, u32[]{:S(2)}) %copy-start.6) | copy-done | bytes 32792
  3.1 0.4 copy.23
  3.5 1.1 %reshape.104 = bf16[4,2,4608]{2,1,0:T(2,128)(2,1)} reshape(bf16[128,12,24]{2,1,0:T(8,128)(2,1)S(1)} %bitcast.62) | data formatting | bytes 147456
  4.7 6.5 %all-to-all-start = ((bf16[4,2,4608]{2,1,0:T(2,128)(2,1)}), bf16[4,2,4608]{2,1,0:T(2,128)(2,1)S(1)}, u32[]{:S(2)}, u32[]{:S(2)}) async-start(bf16[4,2,4608]{2,1,0:T(2,128)(2,1)} %reshape.104), calls=%async_computation | async-start | bytes 147456 | tf_op jit(solution)/shard_map/all_to_all | solution.py:70
  11.3 0.6 %copy-done.7 = bf16[128,128]{1,0:T(8,128)(2,1)S(1)} copy-done((bf16[128,128]{1,0:T(8,128)(2,1)S(1)}, bf16[128,128]{1,0:T(8,128)(2,1)}, u32[]{:S(2)}) %copy-start.7) | copy-done | bytes 32792
  12.1 0.4 copy.26
  12.6 1.1 %reshape.106 = bf16[4,2,4608]{2,1,0:T(2,128)(2,1)} reshape(bf16[128,12,24]{2,1,0:T(8,128)(2,1)S(1)} %bitcast.63) | data formatting | bytes 147456
  13.7 3.2 %all-to-all-done = bf16[4,2,4608]{2,1,0:T(2,128)(2,1)S(1)} async-done(((bf16[4,2,4608]{2,1,0:T(2,128)(2,1)}), bf16[4,2,4608]{2,1,0:T(2,128)(2,1)S(1)}, u32[]{:S(2)}, u32[]{:S(2)}) %all-to-all-start) | async-done | bytes 73760 | tf_op jit(solution)/shard_map/all_to_all | solution.py:70
  16.9 3.3 %all-to-all-start.1 = ((bf16[4,2,4608]{2,1,0:T(2,128)(2,1)}), bf16[4,2,4608]{2,1,0:T(2,128)(2,1)S(1)}, u32[]{:S(2)}, u32[]{:S(2)}) async-start(bf16[4,2,4608]{2,1,0:T(2,128)(2,1)} %reshape.106), calls=%async_computation.1 | async-start | bytes 147456 | tf_op jit(solution)/shard_map/all_to_all | solution.py:69
  20.2 0.6 %reshape.105 = bf16[128,12,24]{2,1,0:T(8,128)(2,1)S(1)} reshape(bf16[4,2,4608]{2,1,0:T(2,128)(2,1)S(1)} %all-to-all-done) | data formatting | bytes 147456
  20.8 0.4 copy.24
  21.2 0.3 copy.25
  21.5 6.3 %all_gather.3 = bf16[48,48,32]{1,0,2:T(8,128)(2,1)S(1)} all-gather(bf16[24,48,32]{1,0,2:T(8,128)(2,1)S(1)} %copy.25), channel_id=1, replica_groups=mesh['trial'=4,'north'=2,'east'=4] {'north'}, dimensions={0}, use_global_device_ids=true | all-gather | bytes 221184 | tf_op jit(solution)/shard_map/all_gather | solution.py:75
  27.8 0.6 %reshape.107 = bf16[128,12,24]{2,1,0:T(8,128)(2,1)S(1)} reshape(bf16[4,2,4608]{2,1,0:T(2,128)(2,1)S(1)} %all-to-all-done.1) | data formatting | bytes 147456
  28.4 0.4 copy.27
  28.8 0.3 copy.28
  29.1 0.3 fusion.1
  29.7 2.0 %collective-permute-start = (bf16[24,12,32]{2,0,1:T(8,128)(2,1)S(1)}, bf16[24,12,32]{2,0,1:T(8,128)(2,1)S(1)}, u32[]{:S(2)}, u32[]{:S(2)}) collective-permute-start(bf16[24,12,32]{2,0,1:T(8,128)(2,1)S(1)} %get-tuple-element.8), channel_id=1, source_target_pairs={{0,1},{1,2},{2,3},{3,0},{4,5},{5,6},{6,7},{7,4},{8,9},{9,10},{10,1... | collective-permute-start | bytes 55304 | tf_op jit(solution)/shard_map/ppermute | solution.py:84
  31.7 2.4 %collective-permute-start.1 = (bf16[24,12,32]{2,0,1:T(8,128)(2,1)S(1)}, bf16[24,12,32]{2,0,1:T(8,128)(2,1)S(1)}, u32[]{:S(2)}, u32[]{:S(2)}) collective-permute-start(bf16[24,12,32]{2,0,1:T(8,128)(2,1)S(1)} %get-tuple-element.7), channel_id=1, source_target_pairs={{0,2},{1,3},{2,0},{3,1},{4,6},{5,7},{6,4},{7,5},{8,10},{9,11},{10,... | collective-permute-start | bytes 55304 | tf_op jit(solution)/shard_map/ppermute | solution.py:84
  34.1 1.5 %collective-permute-start.2 = (bf16[24,12,32]{2,0,1:T(8,128)(2,1)S(1)}, bf16[24,12,32]{2,0,1:T(8,128)(2,1)S(1)}, u32[]{:S(2)}, u32[]{:S(2)}) collective-permute-start(bf16[24,12,32]{2,0,1:T(8,128)(2,1)S(1)} %get-tuple-element.6), channel_id=1, source_target_pairs={{0,3},{1,0},{2,1},{3,2},{4,7},{5,4},{6,5},{7,6},{8,11},{9,8},{10,9... | collective-permute-start | bytes 55304 | tf_op jit(solution)/shard_map/ppermute | solution.py:84
  35.6 0.3 collective-permute-done
  35.9 1.1 %collective-permute-done.1 = bf16[24,12,32]{2,0,1:T(8,128)(2,1)S(1)} collective-permute-done((bf16[24,12,32]{2,0,1:T(8,128)(2,1)S(1)}, bf16[24,12,32]{2,0,1:T(8,128)(2,1)S(1)}, u32[]{:S(2)}, u32[]{:S(2)}) %collective-permute-start.1) | collective-permute-done | bytes 18464 | tf_op jit(solution)/shard_map/ppermute | solution.py:84
  37.0 1.5 %collective-permute-done.2 = bf16[24,12,32]{2,0,1:T(8,128)(2,1)S(1)} collective-permute-done((bf16[24,12,32]{2,0,1:T(8,128)(2,1)S(1)}, bf16[24,12,32]{2,0,1:T(8,128)(2,1)S(1)}, u32[]{:S(2)}, u32[]{:S(2)}) %collective-permute-start.2) | collective-permute-done | bytes 18464 | tf_op jit(solution)/shard_map/ppermute | solution.py:84
  38.6 0.6 %gather_fusion = bf16[4,24,12,32]{3,1,2,0:T(8,128)(2,1)S(1)} fusion(bf16[4,24,12,32]{3,1,2,0:T(8,128)(2,1)S(1)} %pad_maximum_fusion, s32[1024]{0:T(1024)S(1)} %pad_clamp_fusion), kind=kCustom, calls=%fused_computation | custom fusion | bytes 147472 | tf_op jit(solution)/shard_map/gather | solution.py:85
  39.6 0.4 copy.30
  40.0 0.3 reshape.89
  40.3 0.4 copy-done.5
  40.8 0.6 %copy-done.3 = bf16[128,128]{1,0:T(8,128)(2,1)S(1)} copy-done((bf16[128,128]{1,0:T(8,128)(2,1)S(1)}, bf16[128,128]{1,0:T(8,128)(2,1)}, u32[]{:S(2)}) %copy-start.3) | copy-done | bytes 32792
  41.6 0.6 %copy-done.8 = bf16[128,128]{1,0:T(8,128)(2,1)S(1)} copy-done((bf16[128,128]{1,0:T(8,128)(2,1)S(1)}, bf16[128,128]{1,0:T(8,128)(2,1)}, u32[]{:S(2)}) %copy-start.8) | copy-done | bytes 32792
  42.2 0.8 %fusion.14 = bf16[24,12,128]{2,0,1:T(8,128)(2,1)} fusion(f32[24,12,128]{2,0,1:T(8,128)S(1)} %fusion.24, bf16[24,12,128]{2,0,1:T(8,128)(2,1)S(1)} %fusion.22, bf16[128,128]{1,0:T(8,128)(2,1)S(1)} %copy-done.8), kind=kOutput, calls=%fused_computation.19 | convolution fusion | flops 9621504 | bytes 327680 | tf_op jit(solution)/shard_map/ijc,cd->ijd/dot_general | solution.py:46
  (33 shorter events, 2.2 us)
Async XLA Ops:
  0.0 2.1 %copy-start = (bf16[128,128]{1,0:T(8,128)(2,1)S(1)}, bf16[128,128]{1,0:T(8,128)(2,1)}, u32[]{:S(2)}) copy-start(bf16[128,128]{1,0:T(8,128)(2,1)} %param.12) | copy-start | bytes 98308
  0.0 1.1 %copy-start.1 = (bf16[24,12,128]{2,0,1:T(8,128)(2,1)S(1)}, bf16[24,12,128]{2,0,1:T(8,128)(2,1)}, u32[]{:S(2)}) copy-start(bf16[24,12,128]{2,0,1:T(8,128)(2,1)} %param.9) | copy-start | bytes 221188
  1.3 0.7 %copy-start.4 = (f32[128]{0:T(128)S(1)}, f32[128]{0:T(128)}, u32[]{:S(2)}) copy-start(f32[128]{0:T(128)} %param.10) | copy-start | bytes 1540
  2.1 0.8 %copy-start.6 = (bf16[128,128]{1,0:T(8,128)(2,1)S(1)}, bf16[128,128]{1,0:T(8,128)(2,1)}, u32[]{:S(2)}) copy-start(bf16[128,128]{1,0:T(8,128)(2,1)} %param.14) | copy-start | bytes 98308
  4.7 6.5 %copy-start.2 = (bf16[128,128]{1,0:T(8,128)(2,1)S(1)}, bf16[128,128]{1,0:T(8,128)(2,1)}, u32[]{:S(2)}) copy-start(bf16[128,128]{1,0:T(8,128)(2,1)} %param.11) | copy-start | bytes 98308
  4.7 12.2 %all-to-all-start = ((bf16[4,2,4608]{2,1,0:T(2,128)(2,1)}), bf16[4,2,4608]{2,1,0:T(2,128)(2,1)S(1)}, u32[]{:S(2)}, u32[]{:S(2)}) async-start(bf16[4,2,4608]{2,1,0:T(2,128)(2,1)} %reshape.104), calls=%async_computation | async-start | bytes 147456 | tf_op jit(solution)/shard_map/all_to_all | solution.py:70
  11.1 0.8 %copy-start.7 = (bf16[128,128]{1,0:T(8,128)(2,1)S(1)}, bf16[128,128]{1,0:T(8,128)(2,1)}, u32[]{:S(2)}) copy-start(bf16[128,128]{1,0:T(8,128)(2,1)} %param.13) | copy-start | bytes 98308
  16.9 10.9 %all-to-all-start.1 = ((bf16[4,2,4608]{2,1,0:T(2,128)(2,1)}), bf16[4,2,4608]{2,1,0:T(2,128)(2,1)S(1)}, u32[]{:S(2)}, u32[]{:S(2)}) async-start(bf16[4,2,4608]{2,1,0:T(2,128)(2,1)} %reshape.106), calls=%async_computation.1 | async-start | bytes 147456 | tf_op jit(solution)/shard_map/all_to_all | solution.py:69
  29.7 6.2 %collective-permute-start = (bf16[24,12,32]{2,0,1:T(8,128)(2,1)S(1)}, bf16[24,12,32]{2,0,1:T(8,128)(2,1)S(1)}, u32[]{:S(2)}, u32[]{:S(2)}) collective-permute-start(bf16[24,12,32]{2,0,1:T(8,128)(2,1)S(1)} %get-tuple-element.8), channel_id=1, source_target_pairs={{0,1},{1,2},{2,3},{3,0},{4,5},{5,6},{6,7},{7,4},{8,9},{9,10},{10,1... | collective-permute-start | bytes 55304 | tf_op jit(solution)/shard_map/ppermute | solution.py:84
  31.7 5.3 %collective-permute-start.1 = (bf16[24,12,32]{2,0,1:T(8,128)(2,1)S(1)}, bf16[24,12,32]{2,0,1:T(8,128)(2,1)S(1)}, u32[]{:S(2)}, u32[]{:S(2)}) collective-permute-start(bf16[24,12,32]{2,0,1:T(8,128)(2,1)S(1)} %get-tuple-element.7), channel_id=1, source_target_pairs={{0,2},{1,3},{2,0},{3,1},{4,6},{5,7},{6,4},{7,5},{8,10},{9,11},{10,... | collective-permute-start | bytes 55304 | tf_op jit(solution)/shard_map/ppermute | solution.py:84
  34.1 4.4 %collective-permute-start.2 = (bf16[24,12,32]{2,0,1:T(8,128)(2,1)S(1)}, bf16[24,12,32]{2,0,1:T(8,128)(2,1)S(1)}, u32[]{:S(2)}, u32[]{:S(2)}) collective-permute-start(bf16[24,12,32]{2,0,1:T(8,128)(2,1)S(1)} %get-tuple-element.6), channel_id=1, source_target_pairs={{0,3},{1,0},{2,1},{3,2},{4,7},{5,4},{6,5},{7,6},{8,11},{9,8},{10,9... | collective-permute-start | bytes 55304 | tf_op jit(solution)/shard_map/ppermute | solution.py:84
  40.0 0.7 %copy-start.5 = (f32[128]{0:T(128)S(1)}, f32[128]{0:T(128)}, u32[]{:S(2)}) copy-start(f32[128]{0:T(128)} %param.15) | copy-start | bytes 1540
  40.7 0.8 %copy-start.3 = (bf16[128,128]{1,0:T(8,128)(2,1)S(1)}, bf16[128,128]{1,0:T(8,128)(2,1)}, u32[]{:S(2)}) copy-start(bf16[128,128]{1,0:T(8,128)(2,1)} %param.16) | copy-start | bytes 98308
  41.4 0.8 %copy-start.8 = (bf16[128,128]{1,0:T(8,128)(2,1)S(1)}, bf16[128,128]{1,0:T(8,128)(2,1)}, u32[]{:S(2)}) copy-start(bf16[128,128]{1,0:T(8,128)(2,1)} %param.17) | copy-start | bytes 98308
